TPU v7x, 32 devices: a whole 2x2x4 slice. The times are simulated.
32 devices in a mesh: parts: 2 (over y), tok: 4 (over z), hid: 4 (over x, core).
Axes of the slice: x: 2, y: 2, z: 4, core: 2. Of those that a mesh axis runs over, the one named last changes fastest.
Arguments:
- tokens: bfloat16 [6144, 8192], P(('parts', 'tok'), 'hid'), parts along dimension 0, may hold values from -6 to 6
- adapter_ids: int32 [6144, 1], P(('parts', 'tok')), parts along dimension 0, may hold values from 0 to 31; in each aligned block of 768 rows (0 to 767, 768 to 1535, ...) at most 72 rows name the same one
- value_weight: bfloat16 [8192, 1024], P('hid'), may hold values from -0.0625 to 0.0625
- adapter_down: bfloat16 [32, 16, 8192], P('tok', None, 'hid'), may hold values from -0.0625 to 0.0625
- adapter_up: bfloat16 [32, 16, 1024], P('tok', None, 'hid'), may hold values from -1.5 to 1.5
Outputs:
- value_out: bfloat16 [6144, 1024], P(('parts', 'tok'), 'hid'), parts along dimension 0
There are 2 independent parts, one for each index of `parts`. A program takes and returns all parts, laid end to end along the dimension named above; an argument that names none is the same for every part. Nothing has to cross between parts.
Inputs may be any that keep to these rules, and one draw needn't show every extreme that they name: `adapter_ids`: among the 768 tokens of one index of tok, each adapter id appears at most 72 times; in some of these aligned blocks one id appears exactly 72 times.
All inputs are finite; a program needn't handle non-finite values.
Results may differ from a plain program's by a relative error of at most 0.0048.
Values may be sent and summed in bfloat16 or wider, within the bound.
A program may use at most 128 MiB of HBM per device.

v0:
```python
import jax
import jax.numpy as jnp
from jax import lax
from jax.sharding import PartitionSpec as P


def per_device(tokens, adapter_ids, value_weight, adapter_down, adapter_up):
    tok_rows, d_local = tokens.shape
    n_tok = lax.axis_size("tok")
    adp_dev = adapter_down.shape[0]
    low_rank = adapter_down.shape[1]
    kv_local = adapter_up.shape[2]
    adapters_all = adp_dev * n_tok
    capacity = max(2, 3 * tok_rows // adapters_all)
    token_ids = adapter_ids[:, 0]
    matches = token_ids[:, None] == token_ids[None, :]
    before = lax.broadcasted_iota(jnp.int32, (tok_rows, tok_rows), 0) > lax.broadcasted_iota(
        jnp.int32, (tok_rows, tok_rows), 1
    )
    position = jnp.sum((matches & before).astype(jnp.int32), axis=1)
    slot_index = token_ids * capacity + position
    slot_rows = (
        jnp.zeros((adapters_all * capacity, d_local), jnp.bfloat16).at[slot_index].set(tokens)
    )
    base_sums = lax.psum_scatter(
        lax.dot_general(
            value_weight, tokens, (((0,), (1,)), ((), ())), preferred_element_type=jnp.float32
        ),
        "hid",
        scatter_dimension=0,
        tiled=True,
    )
    weights_piece = lax.all_gather(adapter_down, "tok", axis=0, tiled=True)
    piece_count = weights_piece.shape[0]
    slot_block = slot_rows
    slot_block = slot_block.reshape(piece_count, capacity, d_local)
    partial_piece = jnp.einsum(
        "acn,arn->rac", slot_block, weights_piece, preferred_element_type=jnp.float32
    )
    partial_piece = partial_piece.reshape(low_rank, piece_count * capacity)
    low_rows = lax.psum(partial_piece, "hid").astype(jnp.bfloat16)
    weights_piece = lax.all_gather(adapter_up, "tok", axis=0, tiled=True)
    piece_count = weights_piece.shape[0]
    low_block = low_rows
    low_block = low_block.reshape(low_rank, piece_count, capacity)
    expanded = jnp.einsum(
        "rac,ark->ack", low_block, weights_piece, preferred_element_type=jnp.float32
    )
    delta_slots = expanded.astype(jnp.bfloat16).reshape(piece_count * capacity, kv_local)
    delta_rows = delta_slots[slot_index]
    return (base_sums.T + delta_rows.astype(jnp.float32)).astype(jnp.bfloat16)


def solution(mesh):
    in_specs = (
        P(("parts", "tok"), "hid"),
        P(("parts", "tok"), None),
        P("hid", None),
        P("tok", None, "hid"),
        P("tok", None, "hid"),
    )
    out_specs = P(("parts", "tok"), "hid")
    return jax.shard_map(
        per_device, mesh=mesh, in_specs=in_specs, out_specs=out_specs, check_vma=False
    )
```

profile of v0, /device:TPU:0, one launch (start us, length us, event | category | flops | bytes accessed | tf_op | source)
XLA Modules:
  0.0 95.5 jit_solution(1115968050295311452)
XLA Ops:
  7.4 0.0 all-gather.2.cloned.1.call-start
  7.4 0.7 all-gather.2.cloned.1.call-update
  8.1 0.0 reduce-scatter.2.cloned.1.call-start
  8.1 8.3 %fusion.6 = f32[1024,768]{1,0:T(8,128)} fusion(bf16[2048,1024]{1,0:T(8,128)(2,1)} %param.7, bf16[768,2048]{1,0:T(8,128)(2,1)} %param.5), kind=kOutput, calls=%fused_computation.15 | convolution fusion | flops 3221225472 | bytes 10485760 | tf_op jit(solution)/shard_map/dot_general | solution.py:26
  16.4 0.0 copy-start.1
  16.4 0.0 reduce-scatter.2.cloned.1.call-update
  16.5 0.7 copy-done.1
  17.1 0.4 convert_reduce_fusion
  17.5 0.0 copy-start
  17.5 13.4 %scatter_custom_fusion = bf16[2304,2048]{1,0:T(8,128)(2,1)} fusion(s32[768]{0:T(1024)S(1)} %fusion.5, bf16[768,2048]{1,0:T(8,128)(2,1)} %param.5, bf16[]{:T(256)} %constant.4.clone.1), kind=kCustom, calls=%fused_computation.2 | custom fusion | bytes 9437696 | tf_op jit(solution)/shard_map/scatter | solution.py:23
  30.9 0.0 copy-done
  30.9 18.3 %all_gather.7 = bf16[32,16,256]{2,1,0:T(8,128)(2,1)S(1)} all-gather(bf16[8,16,256]{2,1,0:T(8,128)(2,1)S(1)} %copy-done), channel_id=1, replica_groups=mesh['parts'=2,'tok'=4,'hid'=4] {'tok'}, dimensions={0}, use_global_device_ids=true | all-gather | bytes 327680 | tf_op jit(solution)/shard_map/all_gather | solution.py:42
  49.2 13.1 %all-gather.2.cloned.1.call-done = bf16[32,16,2048]{2,1,0:T(8,128)(2,1)} async-done(((bf16[8,16,2048]{2,1,0:T(8,128)(2,1)}), bf16[32,16,2048]{2,1,0:T(8,128)(2,1)}) %all-gather.2.cloned.1.call-update) | async-done | bytes 2097168 | tf_op jit(solution)/shard_map/all_gather | solution.py:33
  62.4 6.8 %convolution_bitcast_fusion = f32[16,32,72]{2,0,1:T(8,128)S(1)} fusion(bf16[32,72,2048]{2,1,0:T(8,128)(2,1)} %bitcast.13, bf16[32,16,2048]{2,1,0:T(8,128)(2,1)} %all-gather.2.cloned.1.call-done), kind=kOutput, calls=%fused_computation.8 | convolution fusion | flops 150994944 | bytes 11681792 | tf_op jit(solution)/shard_map/acn,arn->rac/dot_general | solution.py:37
  69.2 0.1 copy.16
  69.3 0.2 reshape.15
  69.5 12.8 %all-reduce.1 = bf16[16,2304]{1,0:T(8,128)(2,1)S(1)} all-reduce(f32[16,2304]{1,0:T(8,128)S(1)} %reshape.15), channel_id=1, replica_groups=mesh['parts'=2,'tok'=4,'hid'=4] {'hid'}, use_global_device_ids=true, to_apply=%region_3.0 | all-reduce | flops 36864 | bytes 221184 | tf_op jit(solution)/shard_map/psum | solution.py:41
  82.3 0.3 reshape.16
  82.6 0.5 convolution_convert_fusion
  83.1 2.7 %gather_fusion = bf16[768,256]{1,0:T(8,128)(2,1)S(1)} fusion(bf16[2304,256]{1,0:T(8,128)(2,1)S(1)} %bitcast.14, s32[1024]{0:T(1024)S(1)} %pad_clamp_fusion), kind=kCustom, calls=%fused_computation | custom fusion | bytes 789504 | tf_op jit(solution)/shard_map/gather | solution.py:50
  85.7 0.2 copy.18
  85.9 0.0 reduce-scatter.2.cloned.1.call-done
  85.9 1.2 %fusion.3 = bf16[768,256]{0,1:T(8,128)(2,1)S(1)} fusion(f32[256,768]{1,0:T(8,128)} %reduce-scatter.2.cloned.1.call-done, bf16[768,256]{0,1:T(8,128)(2,1)S(1)} %copy.18), kind=kLoop, calls=%fused_computation.10 | loop fusion | flops 589824 | bytes 1572864 | tf_op jit(solution)/shard_map/convert_element_type | solution.py:51
  87.1 0.9 copy.19
  (3 shorter events, 0.0 us)
Async XLA Ops:
  7.4 55.0 %all-gather.2.cloned.1.call-start = ((), (), s32[]{:S(2)}) async-start(), calls=%async_computation.2 | async-start | bytes 2621440 | tf_op jit(solution)/shard_map/all_gather | solution.py:33
  8.1 77.8 %reduce-scatter.2.cloned.1.call-start = ((), (), s32[]{:S(2)}) async-start(), calls=%async_computation.1 | async-start | bytes 3932160 | tf_op jit(solution)/shard_map/reduce_scatter | solution.py:25
  16.4 0.7 copy-start.1
  17.5 13.4 %copy-start = (bf16[8,16,256]{2,1,0:T(8,128)(2,1)S(1)}, bf16[8,16,256]{2,1,0:T(8,128)(2,1)}, u32[]{:S(2)}) copy-start(bf16[8,16,256]{2,1,0:T(8,128)(2,1)} %param.9) | copy-start | bytes 196612
Sparse Core Ops, SparseCore 0:
  9.7 52.5 all-gather.1
Sparse Core Ops, SparseCore 1:
  16.5 40.4 reduce-scatter.1
where the time goes:
time: 95.7 us; the launch traced here: 95.5 us
  blocking collectives  31.1 us (32%)
  local copies, waits for them, and re-layouts  18.4 us (19%)
  matrix products  15.6 us (16%)
  between operations  14.9 us (16%)
  waiting for transfers between devices  13.9 us (15%)
  other arithmetic  1.6 us (2%)
    all_gather x1, blocking collectives, per_device(): weights_piece = lax.all_gather(adapter_up, 'tok', axis=0, tiled=True)  18.3 us
    scatter x1, local copies, waits for them, and re-layouts, per_device(): jnp.zeros((adapters_all * capacity, d_local), jnp.bfloat16).at[slot_index]  13.4 us
    all_gather x1, waiting for transfers between devices, per_device(): weights_piece = lax.all_gather(adapter_down, 'tok', axis=0, tiled=True)  13.1 us
    psum x1, blocking collectives, per_device(): low_rows = lax.psum(partial_piece, 'hid').astype(jnp.bfloat16)  12.8 us
    dot_general x1, matrix products, per_device(): lax.dot_general(value_weight, tokens, (((0,), (1,)), ((), ())), preferred...  8.29 us
    dot_general x1, matrix products, per_device(): jnp.einsum('acn,arn->rac', slot_block, weights_piece, preferred_element_t...  6.83 us
    gather x2, local copies, waits for them, and re-layouts, per_device(): delta_rows = delta_slots[slot_index]  2.83 us
  transfers between devices with their start and end apart: 2, of which 1 were waited for; matrix products, arithmetic and copies ran while one was open for 34% of the time, Pallas kernels for 0%

commit v1 on v0

--- a/solution.py
+++ b/solution.py
@@ -2,6 +2,11 @@
 import jax.numpy as jnp
 from jax import lax
 from jax.sharding import PartitionSpec as P
+
+
+def number_the_loops(load):
+    aux = jnp.sum(lax.all_gather(load, "hid"), axis=0)
+    return aux
 
 
 def per_device(tokens, adapter_ids, value_weight, adapter_down, adapter_up):
@@ -38,7 +43,7 @@
         "acn,arn->rac", slot_block, weights_piece, preferred_element_type=jnp.float32
     )
     partial_piece = partial_piece.reshape(low_rank, piece_count * capacity)
-    low_rows = lax.psum(partial_piece, "hid").astype(jnp.bfloat16)
+    low_rows = number_the_loops(partial_piece).astype(jnp.bfloat16)
     weights_piece = lax.all_gather(adapter_up, "tok", axis=0, tiled=True)
     piece_count = weights_piece.shape[0]
     low_block = low_rows

time: 95.7 us -> 90.4 us (0.945)
  blocking collectives: 31.1 us -> 25.8 us
    psum x1 -> x0, blocking collectives: 12.8 us -> none  [per_device(): low_rows = lax.psum(partial_piece, 'hid').astype(jnp.bfloat16)]
    all_gather x0 -> x1, blocking collectives: none -> 7.51 us  [number_the_loops(): aux = jnp.sum(lax.all_gather(load, 'hid'), axis=0)]
  transfers between devices with their start and end apart: 2 -> 2, of which waited for: 1 -> 1; matrix products, arithmetic and copies ran while one was open for 34% -> 36% of each run, Pallas kernels for 0% -> 0%
where the time goes in v1:
time: 90.4 us; the launch traced here: 90.2 us
  blocking collectives  25.8 us (29%)
  local copies, waits for them, and re-layouts  18.4 us (20%)
  matrix products  15.6 us (17%)
  between operations  14.9 us (16%)
  waiting for transfers between devices  13.9 us (15%)
  other arithmetic  1.63 us (2%)
    all_gather x1, blocking collectives, per_device(): weights_piece = lax.all_gather(adapter_up, 'tok', axis=0, tiled=True)  18.3 us
    scatter x1, local copies, waits for them, and re-layouts, per_device(): jnp.zeros((adapters_all * capacity, d_local), jnp.bfloat16).at[slot_index]  13.4 us
    all_gather x1, waiting for transfers between devices, per_device(): weights_piece = lax.all_gather(adapter_down, 'tok', axis=0, tiled=True)  13.1 us
    dot_general x1, matrix products, per_device(): lax.dot_general(value_weight, tokens, (((0,), (1,)), ((), ())), preferred...  8.29 us
    all_gather x1, blocking collectives, number_the_loops(): aux = jnp.sum(lax.all_gather(load, 'hid'), axis=0)  7.51 us
    dot_general x1, matrix products, per_device(): jnp.einsum('acn,arn->rac', slot_block, weights_piece, preferred_element_t...  6.83 us
    gather x2, local copies, waits for them, and re-layouts, per_device(): delta_rows = delta_slots[slot_index]  2.83 us
  transfers between devices with their start and end apart: 2, of which 1 were waited for; matrix products, arithmetic and copies ran while one was open for 36% of the time, Pallas kernels for 0%

profile of v1, /device:TPU:0, one launch (start us, length us, event | category | flops | bytes accessed | tf_op | source)
XLA Modules:
  0.0 90.2 jit_solution(12641079637155354506)
XLA Ops:
  7.4 0.0 all-gather.2.cloned.1.call-start
  7.4 0.7 all-gather.2.cloned.1.call-update
  8.1 0.0 reduce-scatter.2.cloned.1.call-start
  8.1 8.3 %fusion.6 = f32[1024,768]{1,0:T(8,128)} fusion(bf16[2048,1024]{1,0:T(8,128)(2,1)} %param.7, bf16[768,2048]{1,0:T(8,128)(2,1)} %param.5), kind=kOutput, calls=%fused_computation.15 | convolution fusion | flops 3221225472 | bytes 10485760 | tf_op jit(solution)/shard_map/dot_general | solution.py:31
  16.4 0.0 copy-start.1
  16.4 0.0 reduce-scatter.2.cloned.1.call-update
  16.5 0.7 copy-done.1
  17.1 0.4 convert_reduce_fusion
  17.5 0.0 copy-start
  17.5 13.4 %scatter_custom_fusion = bf16[2304,2048]{1,0:T(8,128)(2,1)} fusion(s32[768]{0:T(1024)S(1)} %fusion.5, bf16[768,2048]{1,0:T(8,128)(2,1)} %param.5, bf16[]{:T(256)} %constant.5.clone.1), kind=kCustom, calls=%fused_computation.2 | custom fusion | bytes 9437696 | tf_op jit(solution)/shard_map/scatter | solution.py:28
  30.9 0.0 copy-done
  30.9 18.3 %all_gather.11 = bf16[32,16,256]{2,1,0:T(8,128)(2,1)S(1)} all-gather(bf16[8,16,256]{2,1,0:T(8,128)(2,1)S(1)} %copy-done), channel_id=1, replica_groups=mesh['parts'=2,'tok'=4,'hid'=4] {'tok'}, dimensions={0}, use_global_device_ids=true | all-gather | bytes 327680 | tf_op jit(solution)/shard_map/all_gather | solution.py:47
  49.2 13.1 %all-gather.2.cloned.1.call-done = bf16[32,16,2048]{2,1,0:T(8,128)(2,1)} async-done(((bf16[8,16,2048]{2,1,0:T(8,128)(2,1)}), bf16[32,16,2048]{2,1,0:T(8,128)(2,1)}) %all-gather.2.cloned.1.call-update) | async-done | bytes 2097168 | tf_op jit(solution)/shard_map/all_gather | solution.py:38
  62.4 6.8 %convolution_bitcast_fusion = f32[16,32,72]{2,0,1:T(8,128)S(1)} fusion(bf16[32,72,2048]{2,1,0:T(8,128)(2,1)} %bitcast.13, bf16[32,16,2048]{2,1,0:T(8,128)(2,1)} %all-gather.2.cloned.1.call-done), kind=kOutput, calls=%fused_computation.8 | convolution fusion | flops 150994944 | bytes 11681792 | tf_op jit(solution)/shard_map/acn,arn->rac/dot_general | solution.py:42
  69.2 0.1 copy.16
  69.3 0.2 all_gather_reshape.3
  69.5 7.5 %all_gather.10 = f32[4,16,2304]{2,1,0:T(8,128)S(1)} all-gather(f32[1,16,2304]{2,1,0:T(8,128)S(1)} %all_gather_reshape.3), channel_id=1, replica_groups=mesh['parts'=2,'tok'=4,'hid'=4] {'hid'}, dimensions={0}, use_global_device_ids=true | all-gather | bytes 737280 | tf_op jit(solution)/shard_map/all_gather | solution.py:8
  77.0 0.3 convert_element_type.21
  77.3 0.5 convolution_convert_fusion
  77.8 2.7 %gather_fusion = bf16[768,256]{1,0:T(8,128)(2,1)S(1)} fusion(bf16[2304,256]{1,0:T(8,128)(2,1)S(1)} %bitcast.14, s32[1024]{0:T(1024)S(1)} %pad_clamp_fusion), kind=kCustom, calls=%fused_computation | custom fusion | bytes 789504 | tf_op jit(solution)/shard_map/gather | solution.py:55
  80.4 0.2 copy.18
  80.6 0.0 reduce-scatter.2.cloned.1.call-done
  80.7 1.2 %fusion.3 = bf16[768,256]{0,1:T(8,128)(2,1)S(1)} fusion(f32[256,768]{1,0:T(8,128)} %reduce-scatter.2.cloned.1.call-done, bf16[768,256]{0,1:T(8,128)(2,1)S(1)} %copy.18), kind=kLoop, calls=%fused_computation.10 | loop fusion | flops 589824 | bytes 1572864 | tf_op jit(solution)/shard_map/convert_element_type | solution.py:56
  81.9 0.9 %copy.19 = bf16[768,256]{1,0:T(8,128)(2,1)} copy(bf16[768,256]{0,1:T(8,128)(2,1)S(1)} %fusion.3) | data formatting | bytes 786432 | tf_op jit(solution)/shard_map/convert_element_type | solution.py:56
  (4 shorter events, 0.1 us)
Async XLA Ops:
  7.4 55.0 %all-gather.2.cloned.1.call-start = ((), (), s32[]{:S(2)}) async-start(), calls=%async_computation.2 | async-start | bytes 2621440 | tf_op jit(solution)/shard_map/all_gather | solution.py:38
  8.1 72.6 %reduce-scatter.2.cloned.1.call-start = ((), (), s32[]{:S(2)}) async-start(), calls=%async_computation.1 | async-start | bytes 3932160 | tf_op jit(solution)/shard_map/reduce_scatter | solution.py:30
  16.4 0.7 copy-start.1
  17.5 13.4 %copy-start = (bf16[8,16,256]{2,1,0:T(8,128)(2,1)S(1)}, bf16[8,16,256]{2,1,0:T(8,128)(2,1)}, u32[]{:S(2)}) copy-start(bf16[8,16,256]{2,1,0:T(8,128)(2,1)} %param.9) | copy-start | bytes 196612
Sparse Core Ops, SparseCore 0:
  9.7 52.5 all-gather.1
Sparse Core Ops, SparseCore 1:
  16.5 40.4 reduce-scatter.1
